TPU v7x, 32 devices: a whole 2x2x4 slice. The times are simulated.
32 devices in a mesh: groups: 2 (over x), seq: 16 (over z, y, core).
Axes of the slice: x: 2, y: 2, z: 4, core: 2. Of those that a mesh axis runs over, the one named last changes fastest.
Arguments:
- query_block: bfloat16 [512, 4096], P(('groups', 'seq')), parts along dimension 0, may hold values from -112 to 112
- cache_keys: bfloat16 [8192, 2048], P(('groups', 'seq')), parts along dimension 0, may hold values from -4 to 4
- stored_values: bfloat16 [8192, 2048], P(('groups', 'seq')), parts along dimension 0, may hold values from -6 to 6
- live_counts: int32 [32], P(('groups', 'seq')), parts along dimension 0, may hold values from 128 to 256
- first_position: int32 [2], P('groups'), parts along dimension 0, may hold values from 0 to 3840
- out_weight: bfloat16 [4096, 5376], P('seq'), may hold values from -0.09375 to 0.09375
Outputs:
- attended: bfloat16 [512, 5376], P(('groups', 'seq')), parts along dimension 0
There are 2 independent parts, one for each index of `groups`. A program takes and returns all parts, laid end to end along the dimension named above; an argument that names none is the same for every part. Nothing has to cross between parts.
Inputs may be any that keep to these rules, and one draw needn't show every extreme that they name: `live_counts`: the live slots of a block are its first ones.
All inputs are finite; a program needn't handle non-finite values.
Results may differ from a plain program's by a relative error of at most 0.0058.
Values may be sent and summed in bfloat16 or wider, within the bound.
No kernel may reach another device: no remote copies, remote signals or barrier semaphores. Data moves between devices by JAX's collectives and lax.ppermute only.
A program may use at most 64 MiB of HBM per device.

v0:
```python
import jax
import jax.numpy as jnp
from jax import lax
from jax.sharding import PartitionSpec as P

QUERY_HEADS = 32
KEY_VALUE_HEADS = 16
HEAD_SIZE = 128
score_scale = 168.0 ** (-0.5)
masked_value = -1e30


def head_partial(query_cols, key_cols, value_cols, allowed, group_width):
    row_count = query_cols.shape[0]
    grouped = query_cols.reshape(row_count, group_width, HEAD_SIZE)
    scores = (
        jnp.einsum("rgd,kd->grk", grouped, key_cols, preferred_element_type=jnp.float32)
        * score_scale
    )
    row_best = jnp.max(jnp.where(allowed[None], scores, masked_value), axis=2)
    shifted = jnp.where(allowed[None], scores - row_best[:, :, None], -jnp.inf)
    weights = jnp.exp(shifted)
    weight_sum = jnp.sum(weights, axis=2)
    safe_total = jnp.where(weight_sum > 0, weight_sum, 1.0)
    weighted = jnp.einsum(
        "grk,kd->grd", weights.astype(jnp.bfloat16), value_cols, preferred_element_type=jnp.float32
    )
    value_partial_sum = (weighted / safe_total[:, :, None]).astype(jnp.bfloat16)
    log_sum_exp = jnp.where(weight_sum > 0, row_best + jnp.log(safe_total), masked_value)
    return (value_partial_sum, log_sum_exp)


def merge_sources(received, totals):
    largest = jnp.max(totals, axis=0)
    scales = jnp.exp(totals - largest[None])
    blended = jnp.sum(scales[..., None] * received.astype(jnp.float32), axis=0)
    return (blended / jnp.sum(scales, axis=0)[..., None]).astype(jnp.bfloat16)


def body(query_block, cache_keys, stored_values, live_counts, first_position, out_weight):
    devices = lax.axis_size("seq")
    source = lax.axis_index("seq")
    key_count = cache_keys.shape[0]
    row_total = query_block.shape[0] * devices
    per_group = QUERY_HEADS // devices
    group_width = QUERY_HEADS // KEY_VALUE_HEADS
    first_key = source * key_count
    live_count = live_counts[0]
    begin_pos = first_position[0]
    key_index = lax.iota(jnp.int32, key_count)
    piece_rows = lax.all_gather(query_block, "seq", axis=0, tiled=True)
    row_count = piece_rows.shape[0]
    query_pos = begin_pos + lax.iota(jnp.int32, row_count)
    allowed = (key_index[None, :] < live_count) & (
        first_key + key_index[None, :] <= query_pos[:, None]
    )

    def single_head(key_value_head):
        query_cols = lax.dynamic_slice_in_dim(
            piece_rows, key_value_head * (group_width * HEAD_SIZE), group_width * HEAD_SIZE, 1
        )
        key_cols = lax.dynamic_slice_in_dim(cache_keys, key_value_head * HEAD_SIZE, HEAD_SIZE, 1)
        value_cols = lax.dynamic_slice_in_dim(
            stored_values, key_value_head * HEAD_SIZE, HEAD_SIZE, 1
        )
        return head_partial(query_cols, key_cols, value_cols, allowed, group_width)

    value_partial_sum, log_sum_exp = lax.map(
        single_head, jnp.arange(KEY_VALUE_HEADS, dtype=jnp.int32)
    )
    value_partial_sum = jnp.transpose(value_partial_sum, (2, 0, 1, 3)).reshape(
        row_count, QUERY_HEADS, HEAD_SIZE
    )
    log_sum_exp = jnp.transpose(log_sum_exp, (2, 0, 1)).reshape(row_count, QUERY_HEADS)
    value_partial_sum, log_sum_exp = (value_partial_sum, log_sum_exp)
    value_partial_sum, log_sum_exp = (value_partial_sum, log_sum_exp)
    received = lax.all_to_all(
        value_partial_sum[None], "seq", split_axis=2, concat_axis=0, tiled=True
    )
    totals = lax.all_to_all(log_sum_exp[None], "seq", split_axis=2, concat_axis=0, tiled=True)
    merged = merge_sources(received, totals)
    flattened = merged.reshape(row_total, per_group * HEAD_SIZE)
    summed = lax.psum_scatter(
        jnp.dot(flattened, out_weight, preferred_element_type=jnp.float32),
        "seq",
        scatter_dimension=0,
        tiled=True,
    )
    return summed.astype(jnp.bfloat16)


def solution(mesh):
    in_specs = (
        P(("groups", "seq"), None),
        P(("groups", "seq"), None),
        P(("groups", "seq"), None),
        P(("groups", "seq")),
        P("groups"),
        P("seq", None),
    )
    out_specs = P(("groups", "seq"), None)
    return jax.shard_map(body, mesh=mesh, in_specs=in_specs, out_specs=out_specs, check_vma=False)
```

profile of v0, /device:TPU:0, one launch (start us, length us, event | category | flops | bytes accessed | tf_op | source)
XLA Modules:
  0.0 307.4 jit_solution(6038253713847439832)
XLA Ops:
  8.7 45.0 %all-gather.2.cloned.1.call-done = bf16[256,4096]{1,0:T(8,128)(2,1)} async-done(((bf16[16,4096]{1,0:T(8,128)(2,1)}), bf16[256,4096]{1,0:T(8,128)(2,1)}) %all-gather.2.cloned.1.call-update) | async-done | bytes 2097168 | tf_op jit(solution)/shard_map/all_gather | solution.py:51
  53.7 97.2 %while.13 = (s32[]{:T(128)}, bf16[16,2,256,128]{3,2,1,0:T(8,128)(2,1)}, f32[16,2,256]{2,1,0:T(2,128)S(1)}, s32[16]{0:T(128)S(1)}, bf16[256,2048]{1,0:T(8,128)(2,...) while((s32[]{:T(128)}, ...), condition=%wide.region_3.4_spmd.clone, body=%wide.region_0.3_spmd.clone.sunk | while | flops 68552712 | bytes 2775577 | solution.py:68
  58.0 1.8 fusion.40
  64.0 1.8 fusion.40
  70.1 1.8 fusion.40
  76.2 1.8 fusion.40
  82.3 1.8 fusion.40
  88.3 1.8 fusion.40
  94.4 1.8 fusion.40
  100.5 1.8 fusion.40
  106.6 1.8 fusion.40
  112.6 1.8 fusion.40
  118.7 1.8 fusion.40
  124.8 1.8 fusion.40
  130.9 1.8 fusion.40
  136.9 1.8 fusion.40
  143.0 1.8 fusion.40
  149.1 1.8 fusion.40
  151.0 9.9 %all_to_all.27 = f32[1,256,32]{1,0,2:T(1,128)S(1)} all-to-all(f32[1,256,32]{1,0,2:T(1,128)S(1)} %broadcast_in_dim_reshape.6), channel_id=1, replica_groups=mesh['groups'=2,'seq'=16] {'seq'}, dimensions={2} | all-to-all | bytes 65536 | tf_op jit(solution)/shard_map/all_to_all | solution.py:80
  160.8 4.4 %all-to-all-start.1 = ((bf16[1,256,32,128]{3,1,0,2:T(8,128)(2,1)}), bf16[1,256,32,128]{3,1,0,2:T(8,128)(2,1)}, u32[]{:S(2)}, u32[]{:S(2)}) async-start(bf16[1,256,32,128]{3,1,0,2:T(8,128)(2,1)} %bitcast.71), calls=%async_computation.1 | async-start | bytes 4194304 | tf_op jit(solution)/shard_map/all_to_all | solution.py:77
  165.4 40.8 %all-to-all-done.1 = bf16[1,256,32,128]{3,1,0,2:T(8,128)(2,1)} async-done(((bf16[1,256,32,128]{3,1,0,2:T(8,128)(2,1)}), bf16[1,256,32,128]{3,1,0,2:T(8,128)(2,1)}, u32[]{:S(2)}, u32[]{:S(2)}) %all-to-all-start.1) | async-done | bytes 2097184 | tf_op jit(solution)/shard_map/all_to_all | solution.py:77
  206.2 2.5 fusion.22
  209.0 3.3 %fusion.26 = f32[256,5376]{1,0:T(8,128)} fusion(bf16[256,256]{0,1:T(8,128)(2,1)S(1)} %bitcast.72, bf16[256,5376]{1,0:T(8,128)(2,1)S(1)} %copy-done), kind=kOutput, calls=%fused_computation.39 | convolution fusion | flops 704643072 | bytes 8388608 | tf_op jit(solution)/shard_map/dot_general | solution.py:84
  212.4 86.6 %reduce-scatter.2.cloned.1.call-done = f32[16,5376]{1,0:T(8,128)} async-done(((f32[256,5376]{1,0:T(8,128)}), f32[16,5376]{1,0:T(8,128)}) %reduce-scatter.2.cloned.1.call-update) | async-done | bytes 344080 | tf_op jit(solution)/shard_map/reduce_scatter | solution.py:83
  (145 shorter events, 50.3 us)
Async XLA Ops:
  6.5 202.5 %copy-start = (bf16[256,5376]{1,0:T(8,128)(2,1)S(1)}, bf16[256,5376]{1,0:T(8,128)(2,1)}, u32[]{:S(2)}) copy-start(bf16[256,5376]{1,0:T(8,128)(2,1)} %param.13) | copy-start | bytes 8257540
  6.5 47.2 %all-gather.2.cloned.1.call-start = ((), (), s32[]{:S(2)}) async-start(), calls=%async_computation.3 | async-start | bytes 2228224 | tf_op jit(solution)/shard_map/all_gather | solution.py:51
  160.8 45.4 %all-to-all-start.1 = ((bf16[1,256,32,128]{3,1,0,2:T(8,128)(2,1)}), bf16[1,256,32,128]{3,1,0,2:T(8,128)(2,1)}, u32[]{:S(2)}, u32[]{:S(2)}) async-start(bf16[1,256,32,128]{3,1,0,2:T(8,128)(2,1)} %bitcast.71), calls=%async_computation.1 | async-start | bytes 4194304 | tf_op jit(solution)/shard_map/all_to_all | solution.py:77
  165.3 133.6 %reduce-scatter.2.cloned.1.call-start = ((), (), s32[]{:S(2)}) async-start(), calls=%async_computation.4 | async-start | bytes 5849088 | tf_op jit(solution)/shard_map/reduce_scatter | solution.py:83
Sparse Core Ops, SparseCore 0:
  9.5 44.1 all-gather.1
  212.5 86.3 reduce-scatter.1
where the time goes:
time: 310 us; the launch traced here: 307 us
  waiting for transfers between devices  173 us (56%)
  matrix products  49.7 us (16%)
  local copies, waits for them, and re-layouts  25.9 us (8%)
  loops' own time  20.5 us (7%)
  between operations  14.9 us (5%)
  blocking collectives  9.87 us (3%)
  other arithmetic  9 us (3%)
  starting transfers between devices  4.47 us (1%)
    reduce_scatter x1, waiting for transfers between devices, body(): lax.psum_scatter(jnp.dot(flattened, out_weight, preferred_element_type=jn...  86.6 us
    all_gather x1, waiting for transfers between devices, body(): piece_rows = lax.all_gather(query_block, 'seq', axis=0, tiled=True)  45 us
    all_to_all x1, waiting for transfers between devices, body(): lax.all_to_all(value_partial_sum[None], 'seq', split_axis=2, concat_axis=...  40.8 us
    dot_general x16, matrix products, head_partial(): jnp.einsum('grk,kd->grd', weights.astype(jnp.bfloat16), value_cols, prefe...  29.2 us
    another operation x1, loops' own time, body(): lax.map(single_head, jnp.arange(KEY_VALUE_HEADS, dtype=jnp.int32))  20.5 us
    dot_general x16, matrix products, head_partial(): jnp.einsum('rgd,kd->grk', grouped, key_cols, preferred_element_type=jnp.f...  17.1 us
    dynamic_slice x32, local copies, waits for them, and re-layouts, single_head(): lax.dynamic_slice_in_dim(piece_rows, key_value_head * (group_width * HEAD...  16.3 us
    all_to_all x1, blocking collectives, body(): lax.all_to_all(log_sum_exp[None], 'seq', split_axis=2, concat_axis=0, til...  9.87 us
  transfers between devices with their start and end apart: 3, of which 3 were waited for; matrix products, arithmetic and copies ran while one was open for 0% of the time, Pallas kernels for 0%

commit v1 on v0

--- a/solution.py
+++ b/solution.py
@@ -48,7 +48,14 @@
     live_count = live_counts[0]
     begin_pos = first_position[0]
     key_index = lax.iota(jnp.int32, key_count)
-    piece_rows = lax.all_gather(query_block, "seq", axis=0, tiled=True)
+    devices_2 = lax.axis_size("seq")
+    route = [(i, (i + 1) % devices_2) for i in range(devices_2)]
+    parts = [query_block]
+    for stride in range(1, devices_2):
+        parts = [lax.ppermute(parts[0], "seq", route), *parts]
+    whole = jnp.concatenate(parts, axis=0)
+    shift = (lax.axis_index("seq") + 1) * parts[-1].shape[0]
+    piece_rows = jnp.roll(whole, shift, axis=0)
     row_count = piece_rows.shape[0]
     query_pos = begin_pos + lax.iota(jnp.int32, row_count)
     allowed = (key_index[None, :] < live_count) & (

time: 310 us -> 401 us (1.29)
  waiting for transfers between devices: 173 us -> 234 us
  local copies, waits for them, and re-layouts: 25.9 us -> 45.4 us
  other arithmetic: 9 us -> 18.1 us
    ppermute x0 -> x15, waiting for transfers between devices: none -> 106 us  [body(): parts = [lax.ppermute(parts[0], 'seq', route), *parts]]
    all_gather x1 -> x0, waiting for transfers between devices: 45 us -> none  [body(): piece_rows = lax.all_gather(query_block, 'seq', axis=0, tiled=True)]
    unnamed x2 -> x67, local copies, waits for them, and re-layouts: 0.01 us -> 17.4 us
    dynamic_update_slice x16, other arithmetic: 0.3 us -> 9.48 us  [body(): lax.map(single_head, jnp.arange(KEY_VALUE_HEADS, dtype=jnp.int32))]
  transfers between devices with their start and end apart: 3 -> 17, of which waited for: 3 -> 17; matrix products, arithmetic and copies ran while one was open for 0% -> 0% of each run, Pallas kernels for 0% -> 0%
where the time goes in v1:
time: 401 us; the launch traced here: 398 us
  waiting for transfers between devices  234 us (58%)
  matrix products  49.8 us (12%)
  local copies, waits for them, and re-layouts  45.4 us (11%)
  loops' own time  21.5 us (5%)
  other arithmetic  18.1 us (5%)
  between operations  15.1 us (4%)
  blocking collectives  9.2 us (2%)
  starting transfers between devices  5 us (1%)
    ppermute x15, waiting for transfers between devices, body(): parts = [lax.ppermute(parts[0], 'seq', route), *parts]  106 us
    reduce_scatter x1, waiting for transfers between devices, body(): lax.psum_scatter(jnp.dot(flattened, out_weight, preferred_element_type=jn...  87 us
    all_to_all x1, waiting for transfers between devices, body(): lax.all_to_all(value_partial_sum[None], 'seq', split_axis=2, concat_axis=...  40.8 us
    dot_general x16, matrix products, head_partial(): jnp.einsum('grk,kd->grd', weights.astype(jnp.bfloat16), value_cols, prefe...  29.3 us
    another operation x1, loops' own time, body(): lax.map(single_head, jnp.arange(KEY_VALUE_HEADS, dtype=jnp.int32))  21.5 us
    unnamed x67, local copies, waits for them, and re-layouts  17.4 us
    dot_general x16, matrix products, head_partial(): jnp.einsum('rgd,kd->grk', grouped, key_cols, preferred_element_type=jnp.f...  17.2 us
    dynamic_slice x32, local copies, waits for them, and re-layouts, single_head(): lax.dynamic_slice_in_dim(piece_rows, key_value_head * (group_width * HEAD...  16.3 us
  transfers between devices with their start and end apart: 17, of which 17 were waited for; matrix products, arithmetic and copies ran while one was open for 0% of the time, Pallas kernels for 0%

profile of v1, /device:TPU:0, one launch (start us, length us, event | category | flops | bytes accessed | tf_op | source)
XLA Modules:
  0.0 398.1 jit_solution(10546637513717142564)
XLA Ops:
  7.0 7.9 %collective-permute-done = bf16[16,4096]{1,0:T(8,128)(2,1)S(1)} collective-permute-done((bf16[16,4096]{1,0:T(8,128)(2,1)}, bf16[16,4096]{1,0:T(8,128)(2,1)S(1)}, u32[]{:S(2)}, u32[]{:S(2)}) %collective-permute-start) | collective-permute-done | bytes 131104 | tf_op jit(solution)/shard_map/ppermute | solution.py:55
  14.9 7.1 %collective-permute-done.1 = bf16[16,4096]{1,0:T(8,128)(2,1)S(1)} collective-permute-done((bf16[16,4096]{1,0:T(8,128)(2,1)S(1)}, bf16[16,4096]{1,0:T(8,128)(2,1)S(1)}, u32[]{:S(2)}, u32[]{:S(2)}) %collective-permute-start.1) | collective-permute-done | bytes 131104 | tf_op jit(solution)/shard_map/ppermute | solution.py:55
  22.0 7.1 %collective-permute-done.2 = bf16[16,4096]{1,0:T(8,128)(2,1)S(1)} collective-permute-done((bf16[16,4096]{1,0:T(8,128)(2,1)S(1)}, bf16[16,4096]{1,0:T(8,128)(2,1)S(1)}, u32[]{:S(2)}, u32[]{:S(2)}) %collective-permute-start.2) | collective-permute-done | bytes 131104 | tf_op jit(solution)/shard_map/ppermute | solution.py:55
  29.1 7.1 %collective-permute-done.3 = bf16[16,4096]{1,0:T(8,128)(2,1)S(1)} collective-permute-done((bf16[16,4096]{1,0:T(8,128)(2,1)S(1)}, bf16[16,4096]{1,0:T(8,128)(2,1)S(1)}, u32[]{:S(2)}, u32[]{:S(2)}) %collective-permute-start.3) | collective-permute-done | bytes 131104 | tf_op jit(solution)/shard_map/ppermute | solution.py:55
  36.2 7.1 %collective-permute-done.4 = bf16[16,4096]{1,0:T(8,128)(2,1)S(1)} collective-permute-done((bf16[16,4096]{1,0:T(8,128)(2,1)S(1)}, bf16[16,4096]{1,0:T(8,128)(2,1)S(1)}, u32[]{:S(2)}, u32[]{:S(2)}) %collective-permute-start.4) | collective-permute-done | bytes 131104 | tf_op jit(solution)/shard_map/ppermute | solution.py:55
  43.3 7.1 %collective-permute-done.5 = bf16[16,4096]{1,0:T(8,128)(2,1)S(1)} collective-permute-done((bf16[16,4096]{1,0:T(8,128)(2,1)S(1)}, bf16[16,4096]{1,0:T(8,128)(2,1)S(1)}, u32[]{:S(2)}, u32[]{:S(2)}) %collective-permute-start.5) | collective-permute-done | bytes 131104 | tf_op jit(solution)/shard_map/ppermute | solution.py:55
  51.0 7.1 %collective-permute-done.6 = bf16[16,4096]{1,0:T(8,128)(2,1)S(1)} collective-permute-done((bf16[16,4096]{1,0:T(8,128)(2,1)S(1)}, bf16[16,4096]{1,0:T(8,128)(2,1)S(1)}, u32[]{:S(2)}, u32[]{:S(2)}) %collective-permute-start.6) | collective-permute-done | bytes 131104 | tf_op jit(solution)/shard_map/ppermute | solution.py:55
  58.7 7.1 %collective-permute-done.7 = bf16[16,4096]{1,0:T(8,128)(2,1)S(1)} collective-permute-done((bf16[16,4096]{1,0:T(8,128)(2,1)S(1)}, bf16[16,4096]{1,0:T(8,128)(2,1)S(1)}, u32[]{:S(2)}, u32[]{:S(2)}) %collective-permute-start.7) | collective-permute-done | bytes 131104 | tf_op jit(solution)/shard_map/ppermute | solution.py:55
  66.5 7.1 %collective-permute-done.8 = bf16[16,4096]{1,0:T(8,128)(2,1)S(1)} collective-permute-done((bf16[16,4096]{1,0:T(8,128)(2,1)S(1)}, bf16[16,4096]{1,0:T(8,128)(2,1)S(1)}, u32[]{:S(2)}, u32[]{:S(2)}) %collective-permute-start.8) | collective-permute-done | bytes 131104 | tf_op jit(solution)/shard_map/ppermute | solution.py:55
  74.2 7.1 %collective-permute-done.9 = bf16[16,4096]{1,0:T(8,128)(2,1)S(1)} collective-permute-done((bf16[16,4096]{1,0:T(8,128)(2,1)S(1)}, bf16[16,4096]{1,0:T(8,128)(2,1)S(1)}, u32[]{:S(2)}, u32[]{:S(2)}) %collective-permute-start.9) | collective-permute-done | bytes 131104 | tf_op jit(solution)/shard_map/ppermute | solution.py:55
  82.0 7.1 %collective-permute-done.10 = bf16[16,4096]{1,0:T(8,128)(2,1)S(1)} collective-permute-done((bf16[16,4096]{1,0:T(8,128)(2,1)S(1)}, bf16[16,4096]{1,0:T(8,128)(2,1)S(1)}, u32[]{:S(2)}, u32[]{:S(2)}) %collective-permute-start.10) | collective-permute-done | bytes 131104 | tf_op jit(solution)/shard_map/ppermute | solution.py:55
  89.7 7.1 %collective-permute-done.11 = bf16[16,4096]{1,0:T(8,128)(2,1)S(1)} collective-permute-done((bf16[16,4096]{1,0:T(8,128)(2,1)S(1)}, bf16[16,4096]{1,0:T(8,128)(2,1)S(1)}, u32[]{:S(2)}, u32[]{:S(2)}) %collective-permute-start.11) | collective-permute-done | bytes 131104 | tf_op jit(solution)/shard_map/ppermute | solution.py:55
  97.5 7.1 %collective-permute-done.12 = bf16[16,4096]{1,0:T(8,128)(2,1)S(1)} collective-permute-done((bf16[16,4096]{1,0:T(8,128)(2,1)S(1)}, bf16[16,4096]{1,0:T(8,128)(2,1)S(1)}, u32[]{:S(2)}, u32[]{:S(2)}) %collective-permute-start.12) | collective-permute-done | bytes 131104 | tf_op jit(solution)/shard_map/ppermute | solution.py:55
  105.9 6.5 %collective-permute-done.13 = bf16[16,4096]{1,0:T(8,128)(2,1)} collective-permute-done((bf16[16,4096]{1,0:T(8,128)(2,1)S(1)}, bf16[16,4096]{1,0:T(8,128)(2,1)}, u32[]{:S(2)}, u32[]{:S(2)}) %collective-permute-start.13) | collective-permute-done | bytes 131104 | tf_op jit(solution)/shard_map/ppermute | solution.py:55
  113.2 6.6 %collective-permute-done.14 = bf16[16,4096]{1,0:T(8,128)(2,1)} collective-permute-done((bf16[16,4096]{1,0:T(8,128)(2,1)}, bf16[16,4096]{1,0:T(8,128)(2,1)}, u32[]{:S(2)}, u32[]{:S(2)}) %collective-permute-start.14) | collective-permute-done | bytes 131104 | tf_op jit(solution)/shard_map/ppermute | solution.py:55
  133.7 107.3 %while.13 = (s32[]{:T(128)}, bf16[16,2,256,128]{3,2,1,0:T(8,128)(2,1)}, f32[16,2,256]{2,1,0:T(2,128)}, s32[16]{0:T(128)S(1)}, bf16[256,2048]{1,0:T(8,128)(2,1)},...) while((s32[]{:T(128)}, ...), condition=%wide.region_3.4_spmd.clone, body=%wide.region_0.3_spmd.clone.sunk | while | flops 68552712 | bytes 2776585 | solution.py:75
  164.8 1.8 fusion.40
  184.9 1.8 fusion.40
  241.8 9.2 %all_to_all.27 = f32[1,256,32]{1,0,2:T(1,128)S(1)} all-to-all(f32[1,256,32]{1,0,2:T(1,128)S(1)} %broadcast_in_dim_reshape.6), channel_id=1, replica_groups=mesh['groups'=2,'seq'=16] {'seq'}, dimensions={2} | all-to-all | bytes 65536 | tf_op jit(solution)/shard_map/all_to_all | solution.py:87
  251.0 4.4 %all-to-all-start.1 = ((bf16[1,256,32,128]{3,1,0,2:T(8,128)(2,1)}), bf16[1,256,32,128]{3,1,0,2:T(8,128)(2,1)}, u32[]{:S(2)}, u32[]{:S(2)}) async-start(bf16[1,256,32,128]{3,1,0,2:T(8,128)(2,1)} %bitcast.71), calls=%async_computation.1 | async-start | bytes 4194304 | tf_op jit(solution)/shard_map/all_to_all | solution.py:84
  255.6 40.8 %all-to-all-done.1 = bf16[1,256,32,128]{3,1,0,2:T(8,128)(2,1)} async-done(((bf16[1,256,32,128]{3,1,0,2:T(8,128)(2,1)}), bf16[1,256,32,128]{3,1,0,2:T(8,128)(2,1)}, u32[]{:S(2)}, u32[]{:S(2)}) %all-to-all-start.1) | async-done | bytes 2097184 | tf_op jit(solution)/shard_map/all_to_all | solution.py:84
  296.4 2.5 fusion.22
  299.2 3.3 fusion.26
  302.6 87.0 %reduce-scatter.2.cloned.1.call-done = f32[16,5376]{1,0:T(8,128)} async-done(((f32[256,5376]{1,0:T(8,128)}), f32[16,5376]{1,0:T(8,128)}) %reduce-scatter.2.cloned.1.call-update) | async-done | bytes 344080 | tf_op jit(solution)/shard_map/reduce_scatter | solution.py:90
  (239 shorter events, 104.4 us)
Async XLA Ops:
  6.5 292.7 %copy-start = (bf16[256,5376]{1,0:T(8,128)(2,1)S(1)}, bf16[256,5376]{1,0:T(8,128)(2,1)}, u32[]{:S(2)}) copy-start(bf16[256,5376]{1,0:T(8,128)(2,1)} %param.13) | copy-start | bytes 8257540
  6.5 125.7 %copy-start.1 = (bf16[16,4096]{1,0:T(8,128)(2,1)S(1)}, bf16[16,4096]{1,0:T(8,128)(2,1)}, u32[]{:S(2)}) copy-start(bf16[16,4096]{1,0:T(8,128)(2,1)} %param.8) | copy-start | bytes 393220
  6.5 8.4 %collective-permute-start = (bf16[16,4096]{1,0:T(8,128)(2,1)}, bf16[16,4096]{1,0:T(8,128)(2,1)S(1)}, u32[]{:S(2)}, u32[]{:S(2)}) collective-permute-start(bf16[16,4096]{1,0:T(8,128)(2,1)} %param.8), channel_id=1, source_target_pairs={{0,1},{1,2},{2,3},{3,4},{4,5},{5,6},{6,7},{7,8},{8,9},{9,10},{10,1... | collective-permute-start | bytes 393224 | tf_op jit(solution)/shard_map/ppermute | solution.py:55
  14.9 7.1 %collective-permute-start.1 = (bf16[16,4096]{1,0:T(8,128)(2,1)S(1)}, bf16[16,4096]{1,0:T(8,128)(2,1)S(1)}, u32[]{:S(2)}, u32[]{:S(2)}) collective-permute-start(bf16[16,4096]{1,0:T(8,128)(2,1)S(1)} %collective-permute-done), channel_id=1, source_target_pairs={{0,1},{1,2},{2,3},{3,4},{4,5},{5,6},{6,7},{7,8},{8,9},{9,10},{10,1... | collective-permute-start | bytes 393224 | tf_op jit(solution)/shard_map/ppermute | solution.py:55
  22.0 7.1 %collective-permute-start.2 = (bf16[16,4096]{1,0:T(8,128)(2,1)S(1)}, bf16[16,4096]{1,0:T(8,128)(2,1)S(1)}, u32[]{:S(2)}, u32[]{:S(2)}) collective-permute-start(bf16[16,4096]{1,0:T(8,128)(2,1)S(1)} %collective-permute-done.1), channel_id=1, source_target_pairs={{0,1},{1,2},{2,3},{3,4},{4,5},{5,6},{6,7},{7,8},{8,9},{9,10},{10,1... | collective-permute-start | bytes 393224 | tf_op jit(solution)/shard_map/ppermute | solution.py:55
  29.1 7.1 %collective-permute-start.3 = (bf16[16,4096]{1,0:T(8,128)(2,1)S(1)}, bf16[16,4096]{1,0:T(8,128)(2,1)S(1)}, u32[]{:S(2)}, u32[]{:S(2)}) collective-permute-start(bf16[16,4096]{1,0:T(8,128)(2,1)S(1)} %collective-permute-done.2), channel_id=1, source_target_pairs={{0,1},{1,2},{2,3},{3,4},{4,5},{5,6},{6,7},{7,8},{8,9},{9,10},{10,1... | collective-permute-start | bytes 393224 | tf_op jit(solution)/shard_map/ppermute | solution.py:55
  36.2 7.1 %collective-permute-start.4 = (bf16[16,4096]{1,0:T(8,128)(2,1)S(1)}, bf16[16,4096]{1,0:T(8,128)(2,1)S(1)}, u32[]{:S(2)}, u32[]{:S(2)}) collective-permute-start(bf16[16,4096]{1,0:T(8,128)(2,1)S(1)} %collective-permute-done.3), channel_id=1, source_target_pairs={{0,1},{1,2},{2,3},{3,4},{4,5},{5,6},{6,7},{7,8},{8,9},{9,10},{10,1... | collective-permute-start | bytes 393224 | tf_op jit(solution)/shard_map/ppermute | solution.py:55
  43.3 7.1 %collective-permute-start.5 = (bf16[16,4096]{1,0:T(8,128)(2,1)S(1)}, bf16[16,4096]{1,0:T(8,128)(2,1)S(1)}, u32[]{:S(2)}, u32[]{:S(2)}) collective-permute-start(bf16[16,4096]{1,0:T(8,128)(2,1)S(1)} %collective-permute-done.4), channel_id=1, source_target_pairs={{0,1},{1,2},{2,3},{3,4},{4,5},{5,6},{6,7},{7,8},{8,9},{9,10},{10,1... | collective-permute-start | bytes 393224 | tf_op jit(solution)/shard_map/ppermute | solution.py:55
  51.0 7.1 %collective-permute-start.6 = (bf16[16,4096]{1,0:T(8,128)(2,1)S(1)}, bf16[16,4096]{1,0:T(8,128)(2,1)S(1)}, u32[]{:S(2)}, u32[]{:S(2)}) collective-permute-start(bf16[16,4096]{1,0:T(8,128)(2,1)S(1)} %collective-permute-done.5), channel_id=1, source_target_pairs={{0,1},{1,2},{2,3},{3,4},{4,5},{5,6},{6,7},{7,8},{8,9},{9,10},{10,1... | collective-permute-start | bytes 393224 | tf_op jit(solution)/shard_map/ppermute | solution.py:55
  58.7 7.1 %collective-permute-start.7 = (bf16[16,4096]{1,0:T(8,128)(2,1)S(1)}, bf16[16,4096]{1,0:T(8,128)(2,1)S(1)}, u32[]{:S(2)}, u32[]{:S(2)}) collective-permute-start(bf16[16,4096]{1,0:T(8,128)(2,1)S(1)} %collective-permute-done.6), channel_id=1, source_target_pairs={{0,1},{1,2},{2,3},{3,4},{4,5},{5,6},{6,7},{7,8},{8,9},{9,10},{10,1... | collective-permute-start | bytes 393224 | tf_op jit(solution)/shard_map/ppermute | solution.py:55
  66.5 7.1 %collective-permute-start.8 = (bf16[16,4096]{1,0:T(8,128)(2,1)S(1)}, bf16[16,4096]{1,0:T(8,128)(2,1)S(1)}, u32[]{:S(2)}, u32[]{:S(2)}) collective-permute-start(bf16[16,4096]{1,0:T(8,128)(2,1)S(1)} %collective-permute-done.7), channel_id=1, source_target_pairs={{0,1},{1,2},{2,3},{3,4},{4,5},{5,6},{6,7},{7,8},{8,9},{9,10},{10,1... | collective-permute-start | bytes 393224 | tf_op jit(solution)/shard_map/ppermute | solution.py:55
  74.2 7.1 %collective-permute-start.9 = (bf16[16,4096]{1,0:T(8,128)(2,1)S(1)}, bf16[16,4096]{1,0:T(8,128)(2,1)S(1)}, u32[]{:S(2)}, u32[]{:S(2)}) collective-permute-start(bf16[16,4096]{1,0:T(8,128)(2,1)S(1)} %collective-permute-done.8), channel_id=1, source_target_pairs={{0,1},{1,2},{2,3},{3,4},{4,5},{5,6},{6,7},{7,8},{8,9},{9,10},{10,1... | collective-permute-start | bytes 393224 | tf_op jit(solution)/shard_map/ppermute | solution.py:55
  82.0 7.1 %collective-permute-start.10 = (bf16[16,4096]{1,0:T(8,128)(2,1)S(1)}, bf16[16,4096]{1,0:T(8,128)(2,1)S(1)}, u32[]{:S(2)}, u32[]{:S(2)}) collective-permute-start(bf16[16,4096]{1,0:T(8,128)(2,1)S(1)} %collective-permute-done.9), channel_id=1, source_target_pairs={{0,1},{1,2},{2,3},{3,4},{4,5},{5,6},{6,7},{7,8},{8,9},{9,10},{10,1... | collective-permute-start | bytes 393224 | tf_op jit(solution)/shard_map/ppermute | solution.py:55
  89.7 7.1 %collective-permute-start.11 = (bf16[16,4096]{1,0:T(8,128)(2,1)S(1)}, bf16[16,4096]{1,0:T(8,128)(2,1)S(1)}, u32[]{:S(2)}, u32[]{:S(2)}) collective-permute-start(bf16[16,4096]{1,0:T(8,128)(2,1)S(1)} %collective-permute-done.10), channel_id=1, source_target_pairs={{0,1},{1,2},{2,3},{3,4},{4,5},{5,6},{6,7},{7,8},{8,9},{9,10},{10,1... | collective-permute-start | bytes 393224 | tf_op jit(solution)/shard_map/ppermute | solution.py:55
  97.5 7.1 %collective-permute-start.12 = (bf16[16,4096]{1,0:T(8,128)(2,1)S(1)}, bf16[16,4096]{1,0:T(8,128)(2,1)S(1)}, u32[]{:S(2)}, u32[]{:S(2)}) collective-permute-start(bf16[16,4096]{1,0:T(8,128)(2,1)S(1)} %collective-permute-done.11), channel_id=1, source_target_pairs={{0,1},{1,2},{2,3},{3,4},{4,5},{5,6},{6,7},{7,8},{8,9},{9,10},{10,1... | collective-permute-start | bytes 393224 | tf_op jit(solution)/shard_map/ppermute | solution.py:55
  105.2 7.2 %collective-permute-start.13 = (bf16[16,4096]{1,0:T(8,128)(2,1)S(1)}, bf16[16,4096]{1,0:T(8,128)(2,1)}, u32[]{:S(2)}, u32[]{:S(2)}) collective-permute-start(bf16[16,4096]{1,0:T(8,128)(2,1)S(1)} %collective-permute-done.12), channel_id=1, source_target_pairs={{0,1},{1,2},{2,3},{3,4},{4,5},{5,6},{6,7},{7,8},{8,9},{9,10},{10,1... | collective-permute-start | bytes 393224 | tf_op jit(solution)/shard_map/ppermute | solution.py:55
  112.4 7.4 %collective-permute-start.14 = (bf16[16,4096]{1,0:T(8,128)(2,1)}, bf16[16,4096]{1,0:T(8,128)(2,1)}, u32[]{:S(2)}, u32[]{:S(2)}) collective-permute-start(bf16[16,4096]{1,0:T(8,128)(2,1)} %collective-permute-done.13), channel_id=1, source_target_pairs={{0,1},{1,2},{2,3},{3,4},{4,5},{5,6},{6,7},{7,8},{8,9},{9,10},{10,1... | collective-permute-start | bytes 393224 | tf_op jit(solution)/shard_map/ppermute | solution.py:55
  113.2 18.8 %copy-start.11 = (bf16[16,4096]{1,0:T(8,128)(2,1)S(1)}, bf16[16,4096]{1,0:T(8,128)(2,1)}, u32[]{:S(2)}) copy-start(bf16[16,4096]{1,0:T(8,128)(2,1)} %copy-done.10) | copy-start | bytes 393220
  113.2 18.8 %copy-start.9 = (bf16[16,4096]{1,0:T(8,128)(2,1)S(1)}, bf16[16,4096]{1,0:T(8,128)(2,1)}, u32[]{:S(2)}) copy-start(bf16[16,4096]{1,0:T(8,128)(2,1)} %copy-done.8) | copy-start | bytes 393220
  113.2 18.8 %copy-start.7 = (bf16[16,4096]{1,0:T(8,128)(2,1)S(1)}, bf16[16,4096]{1,0:T(8,128)(2,1)}, u32[]{:S(2)}) copy-start(bf16[16,4096]{1,0:T(8,128)(2,1)} %copy-done.6) | copy-start | bytes 393220
  113.2 18.8 %copy-start.5 = (bf16[16,4096]{1,0:T(8,128)(2,1)S(1)}, bf16[16,4096]{1,0:T(8,128)(2,1)}, u32[]{:S(2)}) copy-start(bf16[16,4096]{1,0:T(8,128)(2,1)} %copy-done.4) | copy-start | bytes 393220
  113.2 18.9 %copy-start.3 = (bf16[16,4096]{1,0:T(8,128)(2,1)S(1)}, bf16[16,4096]{1,0:T(8,128)(2,1)}, u32[]{:S(2)}) copy-start(bf16[16,4096]{1,0:T(8,128)(2,1)} %copy-done.2) | copy-start | bytes 393220
  251.0 45.4 %all-to-all-start.1 = ((bf16[1,256,32,128]{3,1,0,2:T(8,128)(2,1)}), bf16[1,256,32,128]{3,1,0,2:T(8,128)(2,1)}, u32[]{:S(2)}, u32[]{:S(2)}) async-start(bf16[1,256,32,128]{3,1,0,2:T(8,128)(2,1)} %bitcast.71), calls=%async_computation.1 | async-start | bytes 4194304 | tf_op jit(solution)/shard_map/all_to_all | solution.py:84
  255.5 134.1 %reduce-scatter.2.cloned.1.call-start = ((), (), s32[]{:S(2)}) async-start(), calls=%async_computation.3 | async-start | bytes 5849088 | tf_op jit(solution)/shard_map/reduce_scatter | solution.py:90
  (11 other events, 61.5 us)
Sparse Core Ops, SparseCore 0:
  302.7 86.8 reduce-scatter.1
